TPU v7x, 256 devices: a whole 4x4x8 slice. The times are simulated.
256 devices in a mesh: samp: 16 (over z, x_hi), win: 4 (over x_lo, core), snp: 4 (over y).
Axes of the slice: x: 4 (x_hi: 2, x_lo: 2; x = x_hi * 2 + x_lo), y: 4, z: 8, core: 2. Of those that a mesh axis runs over, the one named last changes fastest.
Arguments:
- dosages: bfloat16 [8192, 16384], P('samp', ('win', 'snp')), may hold values from 0 to 2
Outputs:
- r_squared: float32 [4, 4096, 4096], P('win', 'samp', 'snp')
- band_r_squared: float32 [4, 1024, 4096], P('win', 'samp', 'snp')
All inputs are finite; a program needn't handle non-finite values.
Results may differ from a plain program's by a relative error of at most 0.0003.
Values may be sent and summed in bfloat16 or wider, within the bound.
A program may use at most 128 MiB of HBM per device.

v0:
```python
import jax
import jax.numpy as jnp
from jax import lax
from jax.experimental import pallas as pl
from jax.experimental.pallas import tpu as pltpu
from jax.sharding import PartitionSpec as P

MESH = pl.DeviceIdType.MESH


Z, Y = 8, 4
SAMPLES = 8192
HERE = 1024
HALF = 512
FLOOR = 0.05
POWER = 15
SCALE = 2.0 ** (126.5 / POWER)
FIRST = (0, 64, 128, 192, 256, 320, 384, 448)
ROWS = 64
PARTS = (
    (0, 64, 0, 256), (0, 64, 256, 256), (64, 32, 0, 512), (96, 32, 0, 512), (128, 32, 0, 512), (160, 32, 0, 512),
    (192, 32, 0, 512), (224, 32, 0, 512), (256, 32, 0, 512), (288, 32, 0, 512), (320, 32, 0, 512),
    (352, 32, 0, 512), (384, 32, 0, 512), (416, 32, 0, 512), (448, 32, 0, 512), (480, 32, 0, 512),
    (576, 32, 0, 512), (608, 32, 0, 512), (512, 32, 0, 512), (544, 32, 0, 512),
)

bf16, f32 = jnp.bfloat16, jnp.float32


def coded(w):
    w2 = w * w
    w3 = w2 * w
    w6 = w3 * w3
    w12 = w6 * w6
    return (w12 * w3).astype(bf16)


def decoded(u):
    u = u.astype(f32)
    size = jnp.exp2(jnp.log2(jnp.abs(u)) * (1.0 / POWER))
    return jnp.where(u < 0, -size, size)


def kernel(
    x_hbm, out_hbm, band_hbm,
    x, xt, cols, own, prev, prods, long_in, long_out, short_in, short_out, done,
    st1, st2, st3, st4, rowv, colv, lanes,
    load_sem, x_send, x_recv, p_send, p_recv,
    s1_send, s1_recv, s2_send, s2_recv, s3_send, s3_recv, s4_send, s4_recv,
    d_send, d_recv, r_send, r_recv, c_send, c_recv,
    l_send, l_recv, t_send, t_recv, o_send, o_recv, b_send, b_recv,
):
    samp, win, y = lax.axis_index("samp"), lax.axis_index("win"), lax.axis_index("snp")
    z, hi = samp // 2, samp % 2
    lo, core = win // 2, win % 2

    def dev(z_, hi_, lo_, core_, y_):
        return (2 * z_ + hi_, 2 * lo_ + core_, y_)

    def remote(src, dst, send, recv, to):
        return pltpu.make_async_remote_copy(
            src_ref=src, dst_ref=dst, send_sem=send, recv_sem=recv, device_id=to, device_id_type=MESH
        )

    def go(copy):
        copy.start()

    def bytes_of(ref, sem):
        pltpu.make_async_copy(ref, ref, sem).wait()

    here = dev(z, hi, lo, core, y)
    partner = dev(z, core, 1 - lo, hi, y)
    sibling = dev(z, hi, lo, 1 - core, y)
    up, down = dev(z, hi, lo, core, (y + 1) % Y), dev(z, hi, lo, core, (y + 3) % Y)
    sign = 1 - 2 * core
    fwd, bwd = dev((z + 8 + sign) % Z, hi, lo, core, y), dev((z + 8 - sign) % Z, hi, lo, core, y)
    mine = pl.ds(pl.multiple_of(HALF * core, HALF), HALF)
    by_hi = pl.ds(pl.multiple_of(HALF * hi, HALF), HALF)

    def turn(a):
        xt[pl.ds(128 * a, 128)] = x[:, pl.ds(128 * a, 128)].T

    load = pltpu.make_async_copy(x_hbm, x, load_sem)
    load.start()
    barrier = pltpu.get_barrier_semaphore()
    met = 0
    for k in range(1, Z):
        pl.semaphore_signal(barrier, 1, device_id=dev((z + k) % Z, hi, lo, core, y), device_id_type=MESH)
        met += 1
    for k in range(1, Y):
        pl.semaphore_signal(barrier, 1, device_id=dev(z, hi, lo, core, (y + k) % Y), device_id_type=MESH)
        met += 1
    for k in range(1, 8):
        pl.semaphore_signal(
            barrier, 1, device_id=dev(z, hi ^ (k // 4), lo ^ (k // 2 % 2), core ^ (k % 2), y), device_id_type=MESH
        )
        met += 1
    load.wait()
    turn(0)
    turn(4)

    pl.semaphore_wait(barrier, met)

    def rows_of(q):
        return pl.ds(FIRST[q], ROWS)

    def x_copy(q, i):
        return remote(
            xt.at[pl.ds(HALF * i + FIRST[q], ROWS)], cols.at[2 * y + i, rows_of(q), by_hi],
            x_send, x_recv.at[q], partner,
        )

    def sx(q):
        if q == 2:
            for a in (1, 5, 2, 6, 3, 7):
                turn(a)
        for i in range(2):
            go(x_copy(q, i))

    next_hi, next_lo = 1 - core, jnp.where(core == 0, 1 - lo, lo)

    def prev_copy(c):
        return remote(
            x.at[:, pl.ds(512 * c, 512)], prev.at[by_hi, :], p_send.at[c], p_recv,
            dev(z, next_hi, next_lo, c, y),
        )

    to_self = jnp.logical_and(hi == 0, core == 1)

    def prev_local():
        return pltpu.make_async_copy(x_hbm.at[:, pl.ds(512, 512)], prev.at[by_hi, :], p_recv)

    def pv():
        go(prev_copy(0))
        pl.when(jnp.logical_not(to_self))(lambda: prev_copy(1).start())
        pl.when(to_self)(lambda: prev_local().start())

    def s1_copy(k):
        return remote(
            st1.at[z], st1.at[z], s1_send, s1_recv, dev((z + k) % Z, hi, lo, core, y)
        )

    def d_copy(q, way, i):
        block = cols.at[2 * y + i, rows_of(q), mine]
        return remote(block, block, d_send, d_recv.at[q, way, i], (up, down)[way])

    def r_copy(q, way):
        block = cols.at[2 * ((y + (3, 1)[way]) % Y) + way, rows_of(q), mine]
        return remote(block, block, r_send, r_recv.at[q], (up, down)[way])

    def pair(q, k):
        return cols.at[pl.ds(2 * ((y + k) % Y), 2), rows_of(q), mine]

    def c_copy(q, k):
        return remote(pair(q, k), pair(q, k), c_send, c_recv.at[q, k], sibling)

    def ax(q):
        bytes_of(pair(q, 0), x_recv.at[q])
        go(c_copy(q, 0))

    def da(q):
        for way in range(2):
            go(d_copy(q, way, way))

    def db(q):
        for way in range(2):
            go(d_copy(q, way, 1 - way))

    def re(q, way):
        d_copy(q, way, way).wait_recv()
        go(r_copy(q, way))

    def ne(q, way):
        d_copy(q, way, 1 - way).wait_recv()
        go(c_copy(q, 3 if way == 0 else 1))

    def fa(q):
        bytes_of(pair(q, 0), r_recv.at[q])
        go(c_copy(q, 2))

    def s2_copy(c):
        return remote(
            lanes, st2.at[hi], s2_send, s2_recv, dev(z, core, 1 - lo, c, y)
        )

    def s3_copy(c):
        return remote(
            lanes, st3.at[hi], s3_send.at[c], s3_recv.at[hi], dev(z, next_hi, next_lo, c, y)
        )

    def s4_copy(k):
        return remote(
            st4.at[y], st4.at[y], s4_send, s4_recv, dev(z, hi, lo, core, (y + k) % Y)
        )

    def st_sums():
        @pl.loop(0, 8)
        def _(a):
            v = x[:, pl.ds(pl.multiple_of(128 * a, 128), 128)].astype(f32)
            st1[z, 0, pl.ds(a, 1), :] = jnp.sum(v, axis=0, keepdims=True)
            st1[z, 1, pl.ds(a, 1), :] = jnp.sum(v * v, axis=0, keepdims=True)

        for k in range(1, Z):
            go(s1_copy(k))

    def st_send():
        bytes_of(st1.at[pl.ds(0, Z - 1)], s1_recv)
        total = st1[0]
        for k in range(1, Z):
            total = total + st1[k]
        lanes[0] = total[0]
        lanes[1] = total[1]
        lanes[2] = st1[z, 0]
        for c in range(2):
            go(s2_copy(c))
        go(s3_copy(0))
        pl.when(jnp.logical_not(to_self))(lambda: s3_copy(1).start())

        @pl.when(to_self)
        def _():
            st3[hi] = lanes[...]

    def st_spread():
        bytes_of(st2, s2_recv)
        st4[y] = st2[0] + st2[1]
        for k in range(1, Y):
            go(s4_copy(k))

    def of_sums(parts):
        total, square, local = (parts[k] for k in range(3))
        mean = total * (1.0 / SAMPLES)
        var = jnp.maximum(square * (1.0 / SAMPLES) - mean * mean, FLOOR)
        return mean, 1.0 / jnp.sqrt(var), local

    def st_finish():
        bytes_of(st4.at[pl.ds(0, Y - 1)], s4_recv)

        @pl.loop(0, Y)
        def _(yy):
            mean, inv, local = of_sums(st4[yy])
            e = inv * (SCALE / SAMPLES)
            rowv[yy, 0] = e.T
            rowv[yy, 1] = (local * e).T
            rowv[yy, 2] = (mean * e).T

        def col_vectors(at, parts):
            mean, inv, local = of_sums(parts)
            lanes_of = (inv, mean * inv, (local - HERE * mean) * inv)
            for n, t in enumerate(lanes_of):
                half = jnp.where(core == 0, t[:4], t[4:])
                for j in range(4):
                    colv[at, n, :, pl.ds(128 * j, 128)] = half[j : j + 1]

        col_vectors(0, st4[y])
        for h in range(2):
            there = pltpu.make_async_copy(st3.at[h], st3.at[h], s3_recv.at[h])
            if h == 0:
                pl.when(jnp.logical_not(to_self))(there.wait)
            else:
                there.wait()
        col_vectors(1, st3[0] + st3[1])

    def st(k):
        (st_sums, st_send, st_spread, st_finish)[k]()

    def ow(m):
        for q in range(len(FIRST)):
            if m == FIRST[q] // 128:
                c_copy(q, 0).wait_recv()
        own[:, pl.ds(128 * m, 128)] = cols[2 * y + core, pl.ds(128 * m, 128)].T

    def products(left, right, size, yy, tiles, roots, at, inside, to, part):
        g = lax.dot_general(
            left.reshape(2 * size, HERE), right[:, part], (((1,), (0,)), ((), ())), preferred_element_type=f32
        )
        for i in range(2):
            e, s, m = (rowv[yy, n, pl.ds(inside, size), tiles[i] : tiles[i] + 1] for n in range(3))
            v = [colv[at, n, :, part] for n in range(3)]
            prods[roots[i], pl.ds(to, size), part] = g[size * i : size * i + size] * (e * v[0]) - s * v[1] - m * v[2]

    def pr(q, k, n=None):
        part = pl.ds(0, 512) if n is None else pl.ds(256 * n, 256)
        if q < len(FIRST):
            if k and not n:
                c_copy(q, k).wait_recv()
            yy = (y + k) % Y
            tile, inside = FIRST[q] // 128, FIRST[q] % 128
            left = cols[pl.ds(2 * yy, 2), rows_of(q)]
            products(left, own, ROWS, yy, (tile, 4 + tile), (2 * yy, 2 * yy + 1), 0, inside, FIRST[q], part)
        else:
            if k == 0:
                bytes_of(prev, p_recv)
            left = cols[0:2, pl.ds(128 * k, 128)]
            products(left, prev, 128, 0, (k, 4 + k), (k, 4 + k), 1, 0, 512, part)

    def spot(u):
        row, tall, col, wide = PARTS[u]
        return pl.ds(row, tall), pl.ds(col, wide)

    def l_copy(t, u):
        r, c = spot(u)
        return remote(long_out.at[t, r, c], long_in.at[t, r, c], l_send, l_recv.at[t, u], fwd)

    def t_copy(t, u):
        r, c = spot(u)
        return remote(short_out.at[t, r, c], short_in.at[t, r, c], t_send, t_recv.at[t, u], bwd)

    def L(t, u):
        r, c = spot(u)
        if t:
            l_copy(t - 1, u).wait_recv()
        w = prods[(z + 8 + sign * (4 - t)) % Z, r, c]
        if t:
            w = w + decoded(long_in[t - 1, r, c])
        long_out[t, r, c] = coded(w)
        go(l_copy(t, u))

    def S(t, u):
        r, c = spot(u)
        if t:
            t_copy(t - 1, u).wait_recv()
        w = prods[(z + 8 - sign * (3 - t)) % Z, r, c]
        if t:
            w = w + decoded(short_in[t - 1, r, c])
        short_out[t, r, c] = coded(w)
        go(t_copy(t, u))

    def place(u):
        row, tall, col, wide = PARTS[u]
        span = 256 if row < 512 else 64
        half = (row % 512) // span
        there = pl.ds(row % 512 % span, tall), pl.ds(pl.multiple_of(HALF * core + col, 128), wide)
        return half, there

    def o_copy(u):
        half, (r, c) = place(u)
        return remote(done.at[spot(u)], out_hbm.at[0, r, c], o_send, o_recv, dev(z, half, 1 - lo, hi, y))

    def b_copy(u):
        half, (r, c) = place(u)
        to = dev(z, half, jnp.where(hi == 1, 1 - lo, lo), 1 - hi, y)
        return remote(done.at[spot(u)], band_hbm.at[0, r, c], b_send.at[half], b_recv, to)

    def b_local(u):
        _, (r, c) = place(u)
        return pltpu.make_async_copy(done.at[spot(u)], band_hbm.at[0, r, c], b_recv)

    def F(u):
        r, c = spot(u)
        l_copy(3, u).wait_recv()
        t_copy(2, u).wait_recv()
        w = prods[z, r, c] + decoded(long_in[3, r, c]) + decoded(short_in[2, r, c])
        done[r, c] = w * w * (1.0 / (SCALE * SCALE))
        if PARTS[u][0] < 512:
            go(o_copy(u))
        elif PARTS[u][0] < 576:
            pl.when(jnp.logical_not(to_self))(lambda: b_copy(u).start())
            pl.when(to_self)(lambda: b_local(u).start())
        else:
            go(b_copy(u))

    plan = [
        (sx, 0), (sx, 1), (sx, 2), (sx, 3), (st, 0), (ax, 0), (da, 0), (db, 0), (st, 1), (sx, 4), (sx, 5), (sx, 6),
        (sx, 7), (ax, 1), (da, 1), (ax, 2), (ow, 0), (ax, 3), (re, 0, 0), (re, 0, 1), (db, 1), (st, 2), (da, 2),
        (ne, 0, 0), (ne, 0, 1), (ow, 1), (ax, 4), (re, 1, 0), (re, 1, 1), (db, 2), (da, 3), (ax, 5), (ax, 6),
        (fa, 0), (ow, 2), (ne, 1, 0), (ne, 1, 1), (ax, 7), (st, 3), (pr, 0, 0, 0), (pr, 0, 1, 0), (pr, 0, 2, 0),
        (re, 2, 0), (re, 2, 1), (db, 3), (da, 4), (pr, 0, 3, 0), (ow, 3), (L, 0, 0), (S, 0, 0), (pr, 0, 0, 1),
        (pr, 0, 1, 1), (pr, 0, 2, 1), (pr, 0, 3, 1), (L, 0, 1), (fa, 1), (S, 0, 1), (pr, 1, 0), (pr, 1, 1),
        (pr, 1, 3), (pr, 2, 0), (ne, 2, 0), (ne, 2, 1), (pr, 3, 0), (pr, 1, 2), (L, 0, 2), (S, 0, 2), (L, 0, 3),
        (S, 0, 3), (pr, 4, 0), (pr, 5, 0), (re, 3, 0), (re, 3, 1), (db, 4), (da, 5), (L, 1, 0), (S, 1, 0),
        (pr, 2, 3), (pr, 2, 1), (L, 1, 1), (S, 1, 1), (pr, 6, 0), (fa, 2), (pr, 7, 0), (pv,), (ne, 3, 0), (ne, 3, 1),
        (pr, 2, 2), (L, 1, 2), (S, 1, 2), (L, 0, 4), (S, 0, 4), (L, 0, 5), (S, 0, 5), (L, 1, 3), (S, 1, 3),
        (re, 4, 0), (re, 4, 1), (db, 5), (da, 6), (L, 2, 0), (S, 2, 0), (pr, 3, 1), (pr, 3, 3), (L, 2, 1), (S, 2, 1),
        (fa, 3), (L, 2, 2), (ne, 4, 0), (ne, 4, 1), (S, 2, 2), (pr, 3, 2), (L, 0, 6), (S, 0, 6), (L, 0, 7),
        (S, 0, 7), (L, 1, 4), (S, 1, 4), (re, 5, 0), (re, 5, 1), (db, 6), (da, 7), (L, 1, 5), (S, 1, 5), (pr, 4, 3),
        (pr, 4, 1), (L, 2, 3), (S, 2, 3), (L, 3, 0), (fa, 4), (L, 3, 1), (ne, 5, 0), (ne, 5, 1), (L, 3, 2),
        (pr, 4, 2), (L, 1, 6), (S, 1, 6), (L, 1, 7), (re, 6, 0), (re, 6, 1), (db, 7), (S, 1, 7), (pr, 5, 3),
        (pr, 5, 1), (L, 2, 4), (S, 2, 4), (fa, 5), (L, 2, 5), (S, 2, 5), (L, 3, 3), (F, 0), (L, 0, 8), (S, 0, 8),
        (ne, 6, 0), (ne, 6, 1), (pr, 5, 2), (F, 1), (S, 2, 6), (L, 0, 9), (S, 0, 9), (F, 2), (S, 2, 7), (L, 0, 10),
        (S, 0, 10), (re, 7, 0), (re, 7, 1), (pr, 6, 3), (L, 2, 6), (pr, 6, 1), (L, 2, 7), (fa, 6), (L, 3, 4),
        (L, 3, 5), (S, 1, 8), (F, 3), (ne, 7, 0), (ne, 7, 1), (L, 0, 11), (S, 0, 11), (pr, 6, 2), (L, 1, 8),
        (S, 1, 9), (L, 1, 9), (fa, 7), (pr, 7, 3), (pr, 7, 1), (L, 1, 10), (S, 1, 10), (L, 3, 6), (pr, 7, 2),
        (L, 3, 7), (S, 2, 8), (pr, 8, 0), (F, 4), (S, 1, 11), (L, 0, 12), (S, 0, 12), (pr, 8, 1), (F, 5), (S, 2, 9),
        (L, 0, 13), (S, 0, 13), (L, 1, 11), (pr, 8, 2), (L, 2, 8), (pr, 8, 3), (L, 2, 9), (S, 2, 10), (L, 2, 10),
        (F, 6), (L, 0, 14), (S, 0, 14), (F, 7), (L, 0, 15), (S, 0, 15), (S, 2, 11), (L, 1, 12), (S, 1, 12),
        (L, 1, 13), (L, 2, 11), (S, 1, 13), (L, 3, 8), (L, 3, 9), (S, 1, 14), (L, 3, 10), (S, 1, 15), (L, 1, 14),
        (L, 1, 15), (S, 2, 12), (L, 2, 12), (S, 2, 13), (L, 2, 13), (L, 3, 11), (S, 2, 14), (F, 8), (S, 2, 15),
        (L, 0, 16), (S, 0, 16), (F, 9), (L, 0, 17), (S, 0, 17), (F, 10), (L, 0, 18), (S, 0, 18), (L, 2, 14),
        (L, 2, 15), (L, 3, 12), (L, 3, 13), (F, 11), (L, 0, 19), (S, 0, 19), (S, 1, 16), (L, 1, 16), (L, 1, 17),
        (S, 1, 17), (S, 1, 18), (L, 1, 18), (L, 3, 14), (L, 3, 15), (F, 12), (F, 13), (S, 1, 19), (L, 1, 19),
        (S, 2, 16), (L, 2, 16), (S, 2, 17), (L, 2, 17), (S, 2, 18), (L, 2, 18), (F, 14), (F, 15), (S, 2, 19),
        (L, 2, 19), (L, 3, 16), (L, 3, 17), (L, 3, 18), (L, 3, 19), (F, 16), (F, 17), (F, 18), (F, 19),
    ]
    for step, *at in plan:
        with jax.named_scope("_".join((step.__name__, *map(str, at)))):
            step(*at)

    def ends():
        bytes_of(xt, x_send)
        bytes_of(cols.at[pl.ds(0, 4), :, mine], d_send)
        bytes_of(cols.at[pl.ds(0, 2), :, mine], r_send)
        bytes_of(cols.at[:, :, mine], c_send)
        bytes_of(st1.at[pl.ds(0, Z - 1)], s1_send)
        bytes_of(st4.at[pl.ds(0, 2)], s2_send)
        bytes_of(st4.at[pl.ds(0, Y - 1)], s4_send)
        bytes_of(long_out, l_send)
        bytes_of(short_out, t_send)
        bytes_of(done.at[pl.ds(0, 512)], o_send)
        bytes_of(done.at[pl.ds(576, 64)], b_send.at[1])
        prev_copy(0).wait_send()
        s3_copy(0).wait_send()

        @pl.when(jnp.logical_not(to_self))
        def _():
            prev_copy(1).wait_send()
            s3_copy(1).wait_send()
            bytes_of(done.at[pl.ds(512, 64)], b_send.at[0])

    def outs():
        bytes_of(out_hbm, o_recv)
        bytes_of(band_hbm, b_recv)

    for step in (ends, outs):
        with jax.named_scope(step.__name__):
            step()


def shards(dosages):
    hbm = pl.BlockSpec(memory_space=pl.ANY)
    dma = pltpu.SemaphoreType.DMA
    n = len(FIRST)
    return pl.pallas_call(
        kernel,
        name="ld",
        out_shape=(
            jax.ShapeDtypeStruct((1, 256, 1024), f32),
            jax.ShapeDtypeStruct((1, 64, 1024), f32),
        ),
        in_specs=[pl.BlockSpec(memory_space=pltpu.HBM)],
        out_specs=(hbm, hbm),
        scratch_shapes=[
            pltpu.VMEM((HALF, 1024), bf16),
            pltpu.VMEM((1024, HALF), bf16),
            pltpu.VMEM((Z, 512, HERE), bf16),
            pltpu.VMEM((HERE, 512), bf16),
            pltpu.VMEM((HERE, 512), bf16),
            pltpu.VMEM((Z, 640, 512), f32),
            pltpu.VMEM((4, 640, 512), bf16),
            pltpu.VMEM((4, 640, 512), bf16),
            pltpu.VMEM((3, 640, 512), bf16),
            pltpu.VMEM((3, 640, 512), bf16),
            pltpu.VMEM((640, 512), f32),
            pltpu.VMEM((Z, 2, 8, 128), f32),
            pltpu.VMEM((2, 3, 8, 128), f32),
            pltpu.VMEM((2, 3, 8, 128), f32),
            pltpu.VMEM((Y, 3, 8, 128), f32),
            pltpu.VMEM((Y, 3, 128, 8), f32),
            pltpu.VMEM((2, 3, 1, 512), f32),
            pltpu.VMEM((3, 8, 128), f32),
            dma,
            dma, dma((n,)), dma((2,)), dma,
            dma, dma, dma, dma, dma((2,)), dma((2,)), dma, dma,
            dma, dma((n, 2, 2)), dma, dma((n,)), dma, dma((n, 4)),
            dma, dma((4, len(PARTS))), dma, dma((3, len(PARTS))),
            dma, dma, dma((2,)), dma,
        ],
        compiler_params=pltpu.CompilerParams(has_side_effects=True, collective_id=0, vmem_limit_bytes=44 * 2**20),
    )(pltpu.with_memory_space_constraint(dosages, pltpu.HBM))


def solution(mesh):
    return jax.shard_map(
        shards,
        mesh=mesh,
        in_specs=(P("samp", ("win", "snp")),),
        out_specs=(P("win", "samp", "snp"), P("win", "samp", "snp")),
        check_vma=False,
    )
```

profile of v0, /device:TPU:1, one launch (start us, length us, event | category | flops | bytes accessed | tf_op | source)
XLA Modules:
  0.0 90.3 jit_solution(13604182686033598559)
XLA Ops:
  0.6 88.0 %ld.1 = (f32[1,256,1024]{2,1,0:T(8,128)S(1)}, f32[1,64,1024]{2,1,0:T(8,128)S(1)}) custom-call(bf16[512,1024]{1,0:T(8,128)(2,1)} %x_hbm.1), custom_call_target="tpu_custom_call" | custom-call | tf_op jit(solution)/shard_map/ld/pallas_call | solution.py:432
  88.6 1.0 %copy.5 = f32[1,256,1024]{2,1,0:T(8,128)} copy(f32[1,256,1024]{2,1,0:T(8,128)S(1)} %get-tuple-element.4) | data formatting | bytes 2097152
  89.6 0.7 copy.6
where the time goes:
time: 90.4 us; the launch traced here: 90.3 us
  Pallas kernels  88 us (97%)
  local copies, waits for them, and re-layouts  1.67 us (2%)
    pallas_call x1, Pallas kernels, shards(): pl.pallas_call(kernel, name='ld', out_shape=(jax.ShapeDtypeStruct((1, 256...  88 us

commit v1 on v0

v1 whole, which is shorter than its diff:
```python
import jax
import jax.numpy as jnp
from jax import lax
from jax.experimental import pallas as pl
from jax.experimental.pallas import tpu as pltpu
from jax.sharding import PartitionSpec as P

MESH = pl.DeviceIdType.MESH


Z, Y = 8, 4
SAMPLES = 8192
HERE = 1024
HALF = 512
FLOOR = 0.05
POWER = 15
SCALE = 2.0 ** (126.5 / POWER)
FIRST = (0, 32, 64, 128, 192, 256, 320, 384, 448)
ROWS = (32, 32, 64, 64, 64, 64, 64, 64, 64)
PARTS = (
    (0, 32, 0, 256), (0, 32, 256, 256), (32, 32, 0, 256), (32, 32, 256, 256), (64, 32, 0, 512), (96, 32, 0, 512),
    (128, 32, 0, 512), (160, 32, 0, 512), (192, 32, 0, 512), (224, 32, 0, 512), (256, 32, 0, 512),
    (288, 32, 0, 512), (320, 32, 0, 512), (352, 32, 0, 512), (384, 32, 0, 512), (416, 32, 0, 512),
    (448, 32, 0, 512), (480, 32, 0, 512), (576, 32, 0, 512), (608, 32, 0, 512), (512, 32, 0, 512),
    (544, 32, 0, 512),
)
TURN = sum(row < 128 for row in FIRST)
LONG_AT = (
    (0, 2, 3, 4, 5, 6, 11, 12, 2, 15, 0, 7, 3, 4, 15, 14, 17, 11, 0, 7, 8, 12),
    (1, 0, 8, 9, 10, 13, 5, 16, 8, 9, 5, 1, 6, 16, 9, 3, 1, 13, 2, 15, 6, 16),
    (7, 14, 1, 3, 4, 17, 6, 12, 13, 2, 10, 18, 4, 19, 14, 5, 10, 0, 18, 11, 17, 20),
)
SHORT_AT = (
    (0, 2, 3, 4, 5, 6, 10, 12, 5, 3, 8, 7, 12, 10, 3, 4, 8, 7, 6, 13, 14, 15),
    (1, 0, 7, 8, 9, 11, 4, 0, 9, 6, 11, 2, 5, 0, 9, 1, 2, 11, 10, 12, 16, 3),
)

bf16, f32 = jnp.bfloat16, jnp.float32


def coded(w):
    w2 = w * w
    w3 = w2 * w
    w6 = w3 * w3
    w12 = w6 * w6
    return (w12 * w3).astype(bf16)


def decoded(u):
    u = u.astype(f32)
    size = jnp.exp2(jnp.log2(jnp.abs(u)) * (1.0 / POWER))
    return jnp.where(u < 0, -size, size)


def kernel(
    x_hbm, out_ref, band_ref,
    x, xt, cols, own, prev, prods, long_in, long_out, short_in, short_out, own_out, ends,
    st1, st2, st3, rowv, colv, lanes,
    load_sem, x_send, x_recv, p_send, p_recv,
    s1_send, s1_recv, s2_send, s2_recv, s3_send, s3_recv,
    d_send, d_recv, r_send, r_recv, c_send, c_recv,
    l_send, l_recv, t_send, t_recv, o_send, b_send, e_recv,
):
    samp, win, y = lax.axis_index("samp"), lax.axis_index("win"), lax.axis_index("snp")
    z, hi = samp // 2, samp % 2
    lo, core = win // 2, win % 2

    def dev(z_, hi_, lo_, core_, y_):
        return (2 * z_ + hi_, 2 * lo_ + core_, y_)

    def remote(src, dst, send, recv, to):
        return pltpu.make_async_remote_copy(
            src_ref=src, dst_ref=dst, send_sem=send, recv_sem=recv, device_id=to, device_id_type=MESH
        )

    def go(copy):
        copy.start()

    def bytes_of(ref, sem):
        pltpu.make_async_copy(ref, ref, sem).wait()

    here = dev(z, hi, lo, core, y)
    partner = dev(z, core, 1 - lo, hi, y)
    sibling = dev(z, hi, lo, 1 - core, y)
    up, down = dev(z, hi, lo, core, (y + 1) % Y), dev(z, hi, lo, core, (y + 3) % Y)
    sign = 1 - 2 * core
    fwd, bwd = dev((z + 8 + sign) % Z, hi, lo, core, y), dev((z + 8 - sign) % Z, hi, lo, core, y)
    mine = pl.ds(pl.multiple_of(HALF * core, HALF), HALF)
    by_hi = pl.ds(pl.multiple_of(HALF * hi, HALF), HALF)

    def turn(a):
        xt[pl.ds(128 * a, 128)] = x[:, pl.ds(128 * a, 128)].T

    def load(first, count, k):
        part = pl.ds(128 * first, 128 * count)
        return pltpu.make_async_copy(x_hbm.at[:, part], x.at[:, part], load_sem.at[k])

    loads = [load(0, 1, 0), load(4, 1, 1), load(1, 3, 2), load(5, 3, 3)]
    for copy in loads:
        copy.start()
    barrier = pltpu.get_barrier_semaphore()
    met = 0
    for k in range(1, Z):
        pl.semaphore_signal(barrier, 1, device_id=dev((z + k) % Z, hi, lo, core, y), device_id_type=MESH)
        met += 1
    for k in range(1, Y):
        pl.semaphore_signal(barrier, 1, device_id=dev(z, hi, lo, core, (y + k) % Y), device_id_type=MESH)
        met += 1
    for k in range(1, 8):
        pl.semaphore_signal(
            barrier, 1, device_id=dev(z, hi ^ (k // 4), lo ^ (k // 2 % 2), core ^ (k % 2), y), device_id_type=MESH
        )
        met += 1
    for k in range(1, Y):
        for other in ((core, 0), (core, 1), (1 - core, None)):
            near = dev(z, other[0], 1 - lo, hi if other[1] is None else other[1], (y + k) % Y)
            pl.semaphore_signal(barrier, 1, device_id=near, device_id_type=MESH)
            met += 1
    for dz in (1, Z - 1):
        for k in range(1, 8):
            near = dev((z + dz) % Z, hi ^ (k // 4), lo ^ (k // 2 % 2), core ^ (k % 2), y)
            pl.semaphore_signal(barrier, 1, device_id=near, device_id_type=MESH)
            met += 1
    for n in range(2):
        loads[n].wait()
        turn(4 * n)

    pl.semaphore_wait(barrier, met)

    def rows_of(q):
        return pl.ds(FIRST[q], ROWS[q])

    def x_copy(q, i):
        return remote(
            xt.at[pl.ds(HALF * i + FIRST[q], ROWS[q])], cols.at[2 * y + i, rows_of(q), by_hi],
            x_send, x_recv.at[q], partner,
        )

    def sx(q):
        if q == TURN:
            for a in (1, 5, 2, 6, 3, 7):
                turn(a)
        for i in range(2):
            go(x_copy(q, i))

    next_hi, next_lo = 1 - core, jnp.where(core == 0, 1 - lo, lo)

    def prev_copy(c):
        return remote(
            x.at[:, pl.ds(512 * c, 512)], prev.at[by_hi, :], p_send.at[c], p_recv,
            dev(z, next_hi, next_lo, c, y),
        )

    to_self = jnp.logical_and(hi == 0, core == 1)

    def prev_local():
        return pltpu.make_async_copy(x_hbm.at[:, pl.ds(512, 512)], prev.at[by_hi, :], p_recv)

    def pv():
        go(prev_copy(0))
        pl.when(jnp.logical_not(to_self))(lambda: prev_copy(1).start())
        pl.when(to_self)(lambda: prev_local().start())

    def s1_copy(k):
        return remote(
            st1.at[z], st1.at[z], s1_send, s1_recv, dev((z + k) % Z, hi, lo, core, y)
        )

    def d_copy(q, way, i):
        block = cols.at[2 * y + i, rows_of(q), mine]
        return remote(block, block, d_send, d_recv.at[q, way ^ i], (up, down)[way])

    def r_copy(q, way):
        block = cols.at[2 * ((y + (3, 1)[way]) % Y) + way, rows_of(q), mine]
        return remote(block, block, r_send, r_recv.at[q], (up, down)[way])

    def pair(q, k):
        return cols.at[pl.ds(2 * ((y + k) % Y), 2), rows_of(q), mine]

    def c_copy(q, k):
        return remote(pair(q, k), pair(q, k), c_send, c_recv.at[q, (0, 1, 2, 1)[k]], sibling)

    def ax(q):
        bytes_of(pair(q, 0), x_recv.at[q])
        go(c_copy(q, 0))

    def da(q):
        for way in range(2):
            go(d_copy(q, way, way))

    def db(q):
        for way in range(2):
            go(d_copy(q, way, 1 - way))

    def re(q):
        bytes_of(pair(q, 0), d_recv.at[q, 0])
        for way in range(2):
            go(r_copy(q, way))

    def ne(q):
        bytes_of(pair(q, 0), d_recv.at[q, 1])
        for k in (1, 3):
            go(c_copy(q, k))

    def fa(q):
        bytes_of(pair(q, 0), r_recv.at[q])
        go(c_copy(q, 2))

    def s2_copy(yy, c):
        return remote(lanes, st2.at[y, hi], s2_send, s2_recv, dev(z, core, 1 - lo, c, yy))

    def s3_copy(c):
        return remote(
            lanes, st3.at[hi], s3_send.at[c], s3_recv.at[hi], dev(z, next_hi, next_lo, c, y)
        )

    def st_sums():
        for n in (2, 3):
            loads[n].wait()

        @pl.loop(0, 8)
        def _(a):
            v = x[:, pl.ds(pl.multiple_of(128 * a, 128), 128)].astype(f32)
            st1[z, 0, pl.ds(a, 1), :] = jnp.sum(v, axis=0, keepdims=True)
            st1[z, 1, pl.ds(a, 1), :] = jnp.sum(v * v, axis=0, keepdims=True)

        for k in range(1, Z):
            go(s1_copy(k))

    def st_send():
        bytes_of(st1.at[pl.ds(0, Z - 1)], s1_recv)
        total = st1[0]
        for k in range(1, Z):
            total = total + st1[k]
        lanes[0] = total[0]
        lanes[1] = total[1]
        lanes[2] = st1[z, 0]
        for c in range(2):
            for k in range(Y):
                go(s2_copy((y + k) % Y, c))
        go(s3_copy(0))
        pl.when(jnp.logical_not(to_self))(lambda: s3_copy(1).start())

        @pl.when(to_self)
        def _():
            st3[hi] = lanes[...]

    def of_sums(parts):
        total, square, local = (parts[k] for k in range(3))
        mean = total * (1.0 / SAMPLES)
        var = jnp.maximum(square * (1.0 / SAMPLES) - mean * mean, FLOOR)
        return mean, 1.0 / jnp.sqrt(var), local

    def st_finish():
        bytes_of(st2, s2_recv)

        @pl.loop(0, Y)
        def _(yy):
            mean, inv, local = of_sums(st2[yy, 0] + st2[yy, 1])
            e = inv * (SCALE / SAMPLES)
            rowv[yy, 0] = e.T
            rowv[yy, 1] = (local * e).T
            rowv[yy, 2] = (mean * e).T

        def col_vectors(at, parts):
            mean, inv, local = of_sums(parts)
            lanes_of = (inv, mean * inv, (local - HERE * mean) * inv)
            for n, t in enumerate(lanes_of):
                half = jnp.where(core == 0, t[:4], t[4:])
                for j in range(4):
                    colv[at, n, :, pl.ds(128 * j, 128)] = half[j : j + 1]

        col_vectors(0, st2[y, 0] + st2[y, 1])
        for h in range(2):
            there = pltpu.make_async_copy(st3.at[h], st3.at[h], s3_recv.at[h])
            if h == 0:
                pl.when(jnp.logical_not(to_self))(there.wait)
            else:
                there.wait()
        col_vectors(1, st3[0] + st3[1])

    def st(k):
        (st_sums, st_send, st_finish)[k]()

    def ow(m):
        for q in range(len(FIRST)):
            if m == (FIRST[q] + ROWS[q] - 1) // 128:
                c_copy(q, 0).wait_recv()
        own[:, pl.ds(128 * m, 128)] = cols[2 * y + core, pl.ds(128 * m, 128)].T

    def products(left, right, size, yy, tiles, roots, at, inside, to, part):
        g = lax.dot_general(
            left.reshape(2 * size, HERE), right[:, part], (((1,), (0,)), ((), ())), preferred_element_type=f32
        )
        for i in range(2):
            e, s, m = (rowv[yy, n, pl.ds(inside, size), tiles[i] : tiles[i] + 1] for n in range(3))
            v = [colv[at, n, :, part] for n in range(3)]
            prods[roots[i], pl.ds(to, size), part] = g[size * i : size * i + size] * (e * v[0]) - s * v[1] - m * v[2]

    def main(q, ks, n):
        part = pl.ds(0, 512) if n is None else pl.ds(256 * n, 256)
        tile, inside = FIRST[q] // 128, FIRST[q] % 128
        for k in ks:
            yy = (y + k) % Y
            left = cols[pl.ds(2 * yy, 2), rows_of(q)]
            products(left, own, ROWS[q], yy, (tile, 4 + tile), (2 * yy, 2 * yy + 1), 0, inside, FIRST[q], part)

    def pn(q, n=None):
        if not n:
            bytes_of(cols.at[pl.ds(0, 4), rows_of(q), mine], c_recv.at[q, 1])
        main(q, (0, 1, 3), n)

    def pa(q, n=None):
        main(q, (0, 1, 2, 3), n)

    def pf(q, n=None):
        if not n:
            c_copy(q, 2).wait_recv()
        main(q, (2,), n)

    def pb():
        bytes_of(prev, p_recv)
        for k in range(4):
            left = cols[0:2, pl.ds(128 * k, 128)]
            products(left, prev, 128, 0, (k, 4 + k), (k, 4 + k), 1, 0, 512, pl.ds(0, 512))

    def spot(u):
        row, tall, col, wide = PARTS[u]
        return pl.ds(row, tall), pl.ds(col, wide)

    def half_of(u):
        row = PARTS[u][0]
        return row // 256 if row < 512 else (row - 512) // 64

    def slot(u):
        return sum(half_of(n) == half_of(u) for n in range(u))

    def home(u, z_):
        if PARTS[u][0] < 512:
            return dev(z_, half_of(u), 1 - lo, hi, y)
        return dev(z_, half_of(u), jnp.where(hi == 1, 1 - lo, lo), 1 - hi, y)

    def at_home(u):
        row, tall, col, wide = PARTS[u]
        return pl.ds(row % 256 if row < 512 else 256 + (row - 512) % 64, tall), pl.ds(col, wide)

    def l_copy(t, u):
        r, c = spot(u)
        if t < 3:
            return remote(long_out.at[t, r, c], long_in.at[t, r, c], l_send, l_recv.at[LONG_AT[t][u]], fwd)
        hr, hc = at_home(u)
        return remote(
            long_out.at[t, r, c], ends.at[0, core, hr, hc], l_send, e_recv.at[slot(u), core],
            home(u, (z + 8 + sign) % Z),
        )

    def t_copy(t, u):
        r, c = spot(u)
        if t < 2:
            return remote(short_out.at[t, r, c], short_in.at[t, r, c], t_send, t_recv.at[SHORT_AT[t][u]], bwd)
        hr, hc = at_home(u)
        return remote(
            short_out.at[t, r, c], ends.at[1, core, hr, hc], t_send, e_recv.at[slot(u), core],
            home(u, (z + 8 - sign) % Z),
        )

    def L(t, u):
        r, c = spot(u)
        if t:
            l_copy(t - 1, u).wait_recv()
        w = prods[(z + 8 + sign * (4 - t)) % Z, r, c]
        if t:
            w = w + decoded(long_in[t - 1, r, c])
        long_out[t, r, c] = coded(w)
        go(l_copy(t, u))

    def S(t, u):
        r, c = spot(u)
        if t:
            t_copy(t - 1, u).wait_recv()
        w = prods[(z + 8 - sign * (3 - t)) % Z, r, c]
        if t:
            w = w + decoded(short_in[t - 1, r, c])
        short_out[t, r, c] = coded(w)
        go(t_copy(t, u))

    def local_end(u):
        return PARTS[u][0] >= 512 and half_of(u) == 0

    def O(u):
        r, c = spot(u)
        hr, hc = at_home(u)
        own_out[r, c] = coded(prods[z, r, c])
        main_part = PARTS[u][0] < 512
        copy = remote(
            own_out.at[r, c], ends.at[2, core, hr, hc], o_send if main_part else b_send.at[half_of(u)],
            e_recv.at[slot(u), core], home(u, z),
        )
        if local_end(u):
            pl.when(jnp.logical_not(to_self))(copy.start)

            @pl.when(to_self)
            def _():
                ends[2, 1, hr, hc] = own_out[r, c]
        else:
            copy.start()

    def F(u):
        @pl.when(hi == half_of(u))
        def _():
            row, tall, col, wide = PARTS[u]
            hr, hc = at_home(u)
            for c in range(2):
                def arrived(n):
                    bytes_of(ends.at[0, 0, pl.ds(0, n * tall), pl.ds(0, wide)], e_recv.at[slot(u), c])

                if local_end(u) and c == 1:
                    pl.when(to_self)(lambda: arrived(2))
                    pl.when(jnp.logical_not(to_self))(lambda: arrived(3))
                else:
                    arrived(3)
                w = sum(decoded(ends[n, c, hr, hc]) for n in range(3))
                value = w * w * (1.0 / (SCALE * SCALE))
                there = pl.ds(HALF * c + col, wide)
                if row < 512:
                    out_ref[0, pl.ds(row % 256, tall), there] = value
                else:
                    band_ref[0, pl.ds((row - 512) % 64, tall), there] = value

    plan = [
        (sx, 0), (sx, 1), (sx, 2), (st, 0), (sx, 3), (sx, 4), (sx, 5), (ax, 0), (da, 0), (db, 0), (ax, 1), (da, 1),
        (st, 1), (sx, 6), (sx, 7), (sx, 8), (ax, 2), (ax, 3), (re, 0), (db, 1), (da, 2), (ow, 0), (ne, 0), (ax, 4),
        (re, 1), (db, 2), (da, 3), (ax, 5), (ow, 1), (fa, 0), (ne, 1), (ax, 6), (st, 2), (re, 2), (db, 3), (da, 4),
        (pn, 0, 0), (ax, 7), (fa, 1), (ow, 2), (pf, 0, 0), (L, 0, 0), (S, 0, 0), (pn, 1, 0), (O, 0), (ne, 2),
        (ax, 8), (pv,), (pf, 1, 0), (re, 3), (db, 4), (da, 5), (ow, 3), (pa, 0, 1), (L, 1, 0), (S, 1, 0), (fa, 2),
        (L, 0, 1), (S, 0, 1), (L, 0, 2), (S, 0, 2), (pa, 1, 1), (L, 0, 3), (S, 0, 3), (pn, 2), (ne, 3), (pf, 2),
        (L, 0, 4), (S, 0, 4), (L, 0, 5), (S, 0, 5), (O, 1), (O, 2), (O, 3), (O, 4), (O, 5), (re, 4), (db, 5),
        (da, 6), (L, 2, 0), (S, 2, 0), (pn, 3), (L, 1, 1), (fa, 3), (S, 1, 1), (L, 1, 2), (S, 1, 2), (L, 1, 3),
        (S, 1, 3), (ne, 4), (L, 1, 4), (pf, 3), (S, 1, 4), (L, 0, 6), (S, 0, 6), (L, 0, 7), (L, 1, 5), (S, 1, 5),
        (S, 0, 7), (O, 6), (O, 7), (L, 3, 0), (re, 5), (db, 6), (da, 7), (pn, 4), (L, 2, 1), (S, 2, 1), (L, 2, 2),
        (S, 2, 2), (fa, 4), (L, 2, 3), (S, 2, 3), (L, 2, 4), (S, 2, 4), (ne, 5), (L, 1, 6), (pf, 4), (L, 0, 8),
        (S, 0, 8), (L, 0, 9), (S, 1, 6), (L, 1, 7), (S, 0, 9), (O, 8), (O, 9), (re, 6), (db, 7), (da, 8), (L, 2, 5),
        (S, 2, 5), (pn, 5), (L, 3, 1), (L, 3, 2), (S, 1, 7), (fa, 5), (F, 0), (L, 3, 3), (L, 3, 4), (ne, 6),
        (L, 2, 6), (pf, 5), (S, 1, 8), (L, 0, 10), (S, 0, 10), (L, 0, 11), (S, 0, 11), (O, 10), (L, 1, 8), (O, 11),
        (S, 2, 6), (re, 7), (db, 8), (L, 1, 9), (S, 1, 9), (pn, 6), (L, 2, 7), (fa, 6), (L, 3, 5), (S, 2, 7),
        (ne, 7), (F, 1), (S, 2, 8), (pf, 6), (F, 2), (F, 3), (L, 3, 6), (S, 1, 10), (L, 0, 12), (S, 0, 12),
        (L, 0, 13), (S, 0, 13), (F, 4), (O, 12), (O, 13), (re, 8), (S, 1, 11), (L, 1, 10), (pn, 7), (L, 1, 11),
        (fa, 7), (L, 2, 8), (S, 2, 9), (L, 2, 9), (ne, 8), (L, 3, 7), (pf, 7), (L, 0, 14), (S, 0, 14), (L, 0, 15),
        (S, 0, 15), (S, 2, 10), (O, 14), (O, 15), (S, 1, 12), (fa, 8), (F, 5), (pn, 8), (F, 6), (S, 2, 11),
        (L, 1, 12), (L, 1, 13), (S, 1, 13), (pf, 8), (L, 0, 16), (S, 0, 16), (L, 2, 10), (L, 0, 17), (S, 0, 17),
        (pb,), (L, 3, 8), (L, 2, 11), (S, 1, 14), (S, 1, 15), (L, 3, 9), (L, 0, 18), (S, 0, 18), (L, 0, 19),
        (S, 0, 19), (L, 0, 20), (S, 0, 20), (O, 16), (O, 17), (O, 18), (O, 19), (O, 20), (S, 2, 12), (L, 1, 14),
        (F, 7), (L, 0, 21), (S, 0, 21), (O, 21), (S, 2, 13), (L, 1, 15), (L, 2, 12), (S, 1, 16), (L, 2, 13),
        (S, 1, 17), (S, 2, 14), (L, 1, 16), (L, 3, 10), (S, 2, 15), (L, 1, 17), (S, 1, 18), (S, 1, 19), (L, 3, 11),
        (S, 1, 20), (F, 8), (L, 1, 18), (S, 1, 21), (F, 9), (L, 1, 19), (S, 2, 16), (L, 1, 20), (L, 2, 14),
        (S, 2, 17), (L, 1, 21), (L, 2, 15), (L, 3, 12), (S, 2, 18), (L, 3, 13), (S, 2, 19), (L, 2, 16), (S, 2, 20),
        (S, 2, 21), (L, 2, 17), (F, 10), (L, 2, 18), (F, 11), (L, 2, 19), (L, 2, 20), (L, 3, 14), (L, 2, 21),
        (L, 3, 15), (L, 3, 16), (F, 12), (L, 3, 17), (F, 13), (L, 3, 18), (L, 3, 19), (L, 3, 20), (L, 3, 21),
        (F, 14), (F, 15), (F, 16), (F, 17), (F, 18), (F, 19), (F, 20), (F, 21),
    ]
    for step, *at in plan:
        with jax.named_scope("_".join((step.__name__, *map(str, at)))):
            step(*at)

    def close():
        bytes_of(xt, x_send)
        bytes_of(cols.at[pl.ds(0, 4), :, mine], d_send)
        bytes_of(cols.at[pl.ds(0, 2), :, mine], r_send)
        bytes_of(cols.at[:, :, mine], c_send)
        bytes_of(st1.at[pl.ds(0, Z - 1)], s1_send)
        bytes_of(st2, s2_send)
        bytes_of(long_out, l_send)
        bytes_of(short_out, t_send)
        bytes_of(own_out.at[pl.ds(0, 512)], o_send)
        bytes_of(own_out.at[pl.ds(576, 64)], b_send.at[1])
        prev_copy(0).wait_send()
        s3_copy(0).wait_send()

        @pl.when(jnp.logical_not(to_self))
        def _():
            prev_copy(1).wait_send()
            s3_copy(1).wait_send()
            bytes_of(own_out.at[pl.ds(512, 64)], b_send.at[0])

    with jax.named_scope("close"):
        close()


def shards(dosages):
    vmem = pl.BlockSpec(memory_space=pltpu.VMEM)
    dma = pltpu.SemaphoreType.DMA
    n = len(FIRST)
    return pl.pallas_call(
        kernel,
        name="ld",
        out_shape=(
            jax.ShapeDtypeStruct((1, 256, 1024), f32),
            jax.ShapeDtypeStruct((1, 64, 1024), f32),
        ),
        in_specs=[pl.BlockSpec(memory_space=pltpu.HBM)],
        out_specs=(vmem, vmem),
        scratch_shapes=[
            pltpu.VMEM((HALF, 1024), bf16),
            pltpu.VMEM((1024, HALF), bf16),
            pltpu.VMEM((Z, 512, HERE), bf16),
            pltpu.VMEM((HERE, 512), bf16),
            pltpu.VMEM((HERE, 512), bf16),
            pltpu.VMEM((Z, 640, 512), f32),
            pltpu.VMEM((3, 640, 512), bf16),
            pltpu.VMEM((4, 640, 512), bf16),
            pltpu.VMEM((2, 640, 512), bf16),
            pltpu.VMEM((3, 640, 512), bf16),
            pltpu.VMEM((640, 512), bf16),
            pltpu.VMEM((3, 2, 320, 512), bf16),
            pltpu.VMEM((Z, 2, 8, 128), f32),
            pltpu.VMEM((Y, 2, 3, 8, 128), f32),
            pltpu.VMEM((2, 3, 8, 128), f32),
            pltpu.VMEM((Y, 3, 128, 8), f32),
            pltpu.VMEM((2, 3, 1, 512), f32),
            pltpu.VMEM((3, 8, 128), f32),
            dma((4,)),
            dma, dma((n,)), dma((2,)), dma,
            dma, dma, dma, dma, dma((2,)), dma((2,)),
            dma, dma((n, 2)), dma, dma((n,)), dma, dma((n, 3)),
            dma, dma((1 + max(map(max, LONG_AT)),)), dma, dma((1 + max(map(max, SHORT_AT)),)),
            dma, dma((2,)), dma((len(PARTS), 2)),
        ],
        compiler_params=pltpu.CompilerParams(has_side_effects=True, collective_id=0, vmem_limit_bytes=44 * 2**20),
    )(pltpu.with_memory_space_constraint(dosages, pltpu.HBM))


def solution(mesh):
    return jax.shard_map(
        shards,
        mesh=mesh,
        in_specs=(P("samp", ("win", "snp")),),
        out_specs=(P("win", "samp", "snp"), P("win", "samp", "snp")),
        check_vma=False,
    )
```

time: 90.4 us -> 86.6 us (0.958)
  Pallas kernels: 88 us -> 84.2 us
    pallas_call x1, Pallas kernels: 88 us -> 84.2 us  [shards(): pl.pallas_call(kernel, name='ld', out_shape=(jax.ShapeDtypeStruct((1, 256...]
where the time goes in v1:
time: 86.6 us; the launch traced here: 86.5 us
  Pallas kernels  84.2 us (97%)
  local copies, waits for them, and re-layouts  1.67 us (2%)
    pallas_call x1, Pallas kernels, shards(): pl.pallas_call(kernel, name='ld', out_shape=(jax.ShapeDtypeStruct((1, 256...  84.2 us

profile of v1, /device:TPU:1, one launch (start us, length us, event | category | flops | bytes accessed | tf_op | source)
XLA Modules:
  0.0 86.5 jit_solution(3841715798145265064)
XLA Ops:
  0.6 84.2 %ld.1 = (f32[1,256,1024]{2,1,0:T(8,128)S(1)}, f32[1,64,1024]{2,1,0:T(8,128)S(1)}) custom-call(bf16[512,1024]{1,0:T(8,128)(2,1)} %x_hbm.1), custom_call_target="tpu_custom_call" | custom-call | tf_op jit(solution)/shard_map/ld/pallas_call | solution.py:493
  84.9 1.0 %copy.5 = f32[1,256,1024]{2,1,0:T(8,128)} copy(f32[1,256,1024]{2,1,0:T(8,128)S(1)} %get-tuple-element.4) | data formatting | bytes 2097152
  85.8 0.7 copy.6

commit v2 on v1

--- a/solution.py
+++ b/solution.py
@@ -15,24 +15,34 @@
 FLOOR = 0.05
 POWER = 15
 SCALE = 2.0 ** (126.5 / POWER)
-FIRST = (0, 32, 64, 128, 192, 256, 320, 384, 448)
-ROWS = (32, 32, 64, 64, 64, 64, 64, 64, 64)
+FIRST = (0, 64, 128, 192, 256, 320, 384, 448)
+ROWS = (64, 64, 64, 64, 64, 64, 64, 64)
 PARTS = (
-    (0, 32, 0, 256), (0, 32, 256, 256), (32, 32, 0, 256), (32, 32, 256, 256), (64, 32, 0, 512), (96, 32, 0, 512),
-    (128, 32, 0, 512), (160, 32, 0, 512), (192, 32, 0, 512), (224, 32, 0, 512), (256, 32, 0, 512),
-    (288, 32, 0, 512), (320, 32, 0, 512), (352, 32, 0, 512), (384, 32, 0, 512), (416, 32, 0, 512),
-    (448, 32, 0, 512), (480, 32, 0, 512), (576, 32, 0, 512), (608, 32, 0, 512), (512, 32, 0, 512),
-    (544, 32, 0, 512),
+    (0, 64, 0, 256), (0, 64, 256, 256), (64, 64, 0, 256), (64, 64, 256, 256), (128, 32, 0, 512), (160, 32, 0, 512),
+    (192, 32, 0, 512), (224, 32, 0, 512), (256, 32, 0, 512), (288, 32, 0, 512), (320, 32, 0, 512),
+    (352, 32, 0, 512), (384, 32, 0, 512), (416, 32, 0, 512), (448, 32, 0, 512), (480, 32, 0, 512),
+    (576, 32, 0, 512), (608, 32, 0, 512), (512, 32, 0, 512), (544, 32, 0, 512),
 )
+ENDS = max(sum((r // 256 if r < 512 else (r - 512) // 64) == h for r, _, _, _ in PARTS) for h in range(2))
 TURN = sum(row < 128 for row in FIRST)
 LONG_AT = (
-    (0, 2, 3, 4, 5, 6, 11, 12, 2, 15, 0, 7, 3, 4, 15, 14, 17, 11, 0, 7, 8, 12),
-    (1, 0, 8, 9, 10, 13, 5, 16, 8, 9, 5, 1, 6, 16, 9, 3, 1, 13, 2, 15, 6, 16),
-    (7, 14, 1, 3, 4, 17, 6, 12, 13, 2, 10, 18, 4, 19, 14, 5, 10, 0, 18, 11, 17, 20),
+    (0, 1, 3, 5, 7, 8, 11, 12, 8, 6, 1, 2, 11, 12, 8, 16, 6, 7, 9, 17),
+    (2, 4, 0, 1, 2, 3, 5, 9, 3, 10, 14, 15, 18, 1, 10, 13, 4, 11, 12, 14),
+    (6, 9, 10, 4, 0, 7, 13, 4, 0, 5, 2, 3, 19, 0, 6, 5, 16, 8, 15, 20),
 )
 SHORT_AT = (
-    (0, 2, 3, 4, 5, 6, 10, 12, 5, 3, 8, 7, 12, 10, 3, 4, 8, 7, 6, 13, 14, 15),
-    (1, 0, 7, 8, 9, 11, 4, 0, 9, 6, 11, 2, 5, 0, 9, 1, 2, 11, 10, 12, 16, 3),
+    (0, 1, 3, 5, 6, 7, 2, 8, 5, 4, 10, 11, 8, 1, 6, 0, 12, 7, 13, 14),
+    (2, 4, 0, 1, 3, 9, 0, 6, 7, 2, 9, 3, 4, 5, 10, 11, 2, 15, 9, 1),
+)
+SIDE_AT = (
+    (0, 2, 5, 8, 10, 11, 4, 7),
+    (1, 4, 7, 9, 1, 3, 6, 0),
+    (3, 6, 0, 2, 5, 8, 10, 11),
+)
+CORE_AT = (
+    (0, 1, 2, 3, 4, 1, 2, 5),
+    (0, 6, 1, 3, 1, 3, 1, 3),
+    (3, 0, 2, 0, 2, 0, 2, 0),
 )
 
 bf16, f32 = jnp.bfloat16, jnp.float32
@@ -58,7 +68,7 @@
     st1, st2, st3, rowv, colv, lanes,
     load_sem, x_send, x_recv, p_send, p_recv,
     s1_send, s1_recv, s2_send, s2_recv, s3_send, s3_recv,
-    d_send, d_recv, r_send, r_recv, c_send, c_recv,
+    d_send, d_recv, r_send, c_send, c_recv,
     l_send, l_recv, t_send, t_recv, o_send, b_send, e_recv,
 ):
     samp, win, y = lax.axis_index("samp"), lax.axis_index("win"), lax.axis_index("snp")
@@ -99,33 +109,16 @@
     for copy in loads:
         copy.start()
     barrier = pltpu.get_barrier_semaphore()
-    met = 0
-    for k in range(1, Z):
-        pl.semaphore_signal(barrier, 1, device_id=dev((z + k) % Z, hi, lo, core, y), device_id_type=MESH)
-        met += 1
-    for k in range(1, Y):
-        pl.semaphore_signal(barrier, 1, device_id=dev(z, hi, lo, core, (y + k) % Y), device_id_type=MESH)
-        met += 1
-    for k in range(1, 8):
-        pl.semaphore_signal(
-            barrier, 1, device_id=dev(z, hi ^ (k // 4), lo ^ (k // 2 % 2), core ^ (k % 2), y), device_id_type=MESH
-        )
-        met += 1
-    for k in range(1, Y):
-        for other in ((core, 0), (core, 1), (1 - core, None)):
-            near = dev(z, other[0], 1 - lo, hi if other[1] is None else other[1], (y + k) % Y)
-            pl.semaphore_signal(barrier, 1, device_id=near, device_id_type=MESH)
-            met += 1
-    for dz in (1, Z - 1):
-        for k in range(1, 8):
-            near = dev((z + dz) % Z, hi ^ (k // 4), lo ^ (k // 2 % 2), core ^ (k % 2), y)
-            pl.semaphore_signal(barrier, 1, device_id=near, device_id_type=MESH)
-            met += 1
+    greeted = [dev((z + k) % Z, hi, lo, core, y) for k in range(1, Z)]
+    greeted += [dev(z, hi, lo, c, (y + k) % Y) for k in range(1, Y) for c in range(2)]
+    greeted += [dev(z, hi ^ (k // 4), lo ^ (k // 2 % 2), core ^ (k % 2), y) for k in range(1, 8)]
+    for near in greeted:
+        pl.semaphore_signal(barrier, 1, device_id=near, device_id_type=MESH)
     for n in range(2):
         loads[n].wait()
         turn(4 * n)
 
-    pl.semaphore_wait(barrier, met)
+    pl.semaphore_wait(barrier, len(greeted))
 
     def rows_of(q):
         return pl.ds(FIRST[q], ROWS[q])
@@ -168,17 +161,17 @@
 
     def d_copy(q, way, i):
         block = cols.at[2 * y + i, rows_of(q), mine]
-        return remote(block, block, d_send, d_recv.at[q, way ^ i], (up, down)[way])
+        return remote(block, block, d_send, d_recv.at[SIDE_AT[way ^ i][q]], (up, down)[way])
 
     def r_copy(q, way):
         block = cols.at[2 * ((y + (3, 1)[way]) % Y) + way, rows_of(q), mine]
-        return remote(block, block, r_send, r_recv.at[q], (up, down)[way])
+        return remote(block, block, r_send, d_recv.at[SIDE_AT[2][q]], (up, down)[way])
 
     def pair(q, k):
         return cols.at[pl.ds(2 * ((y + k) % Y), 2), rows_of(q), mine]
 
     def c_copy(q, k):
-        return remote(pair(q, k), pair(q, k), c_send, c_recv.at[q, (0, 1, 2, 1)[k]], sibling)
+        return remote(pair(q, k), pair(q, k), c_send, c_recv.at[CORE_AT[(0, 1, 2, 1)[k]][q]], sibling)
 
     def ax(q):
         bytes_of(pair(q, 0), x_recv.at[q])
@@ -193,17 +186,17 @@
             go(d_copy(q, way, 1 - way))
 
     def re(q):
-        bytes_of(pair(q, 0), d_recv.at[q, 0])
+        bytes_of(pair(q, 0), d_recv.at[SIDE_AT[0][q]])
         for way in range(2):
             go(r_copy(q, way))
 
     def ne(q):
-        bytes_of(pair(q, 0), d_recv.at[q, 1])
+        bytes_of(pair(q, 0), d_recv.at[SIDE_AT[1][q]])
         for k in (1, 3):
             go(c_copy(q, k))
 
     def fa(q):
-        bytes_of(pair(q, 0), r_recv.at[q])
+        bytes_of(pair(q, 0), d_recv.at[SIDE_AT[2][q]])
         go(c_copy(q, 2))
 
     def s2_copy(yy, c):
@@ -254,8 +247,7 @@
     def st_finish():
         bytes_of(st2, s2_recv)
 
-        @pl.loop(0, Y)
-        def _(yy):
+        for yy in range(Y):
             mean, inv, local = of_sums(st2[yy, 0] + st2[yy, 1])
             e = inv * (SCALE / SAMPLES)
             rowv[yy, 0] = e.T
@@ -307,7 +299,7 @@
 
     def pn(q, n=None):
         if not n:
-            bytes_of(cols.at[pl.ds(0, 4), rows_of(q), mine], c_recv.at[q, 1])
+            bytes_of(cols.at[pl.ds(0, 4), rows_of(q), mine], c_recv.at[CORE_AT[1][q]])
         main(q, (0, 1, 3), n)
 
     def pa(q, n=None):
@@ -428,35 +420,32 @@
                     band_ref[0, pl.ds((row - 512) % 64, tall), there] = value
 
     plan = [
-        (sx, 0), (sx, 1), (sx, 2), (st, 0), (sx, 3), (sx, 4), (sx, 5), (ax, 0), (da, 0), (db, 0), (ax, 1), (da, 1),
-        (st, 1), (sx, 6), (sx, 7), (sx, 8), (ax, 2), (ax, 3), (re, 0), (db, 1), (da, 2), (ow, 0), (ne, 0), (ax, 4),
-        (re, 1), (db, 2), (da, 3), (ax, 5), (ow, 1), (fa, 0), (ne, 1), (ax, 6), (st, 2), (re, 2), (db, 3), (da, 4),
-        (pn, 0, 0), (ax, 7), (fa, 1), (ow, 2), (pf, 0, 0), (L, 0, 0), (S, 0, 0), (pn, 1, 0), (O, 0), (ne, 2),
-        (ax, 8), (pv,), (pf, 1, 0), (re, 3), (db, 4), (da, 5), (ow, 3), (pa, 0, 1), (L, 1, 0), (S, 1, 0), (fa, 2),
-        (L, 0, 1), (S, 0, 1), (L, 0, 2), (S, 0, 2), (pa, 1, 1), (L, 0, 3), (S, 0, 3), (pn, 2), (ne, 3), (pf, 2),
-        (L, 0, 4), (S, 0, 4), (L, 0, 5), (S, 0, 5), (O, 1), (O, 2), (O, 3), (O, 4), (O, 5), (re, 4), (db, 5),
-        (da, 6), (L, 2, 0), (S, 2, 0), (pn, 3), (L, 1, 1), (fa, 3), (S, 1, 1), (L, 1, 2), (S, 1, 2), (L, 1, 3),
-        (S, 1, 3), (ne, 4), (L, 1, 4), (pf, 3), (S, 1, 4), (L, 0, 6), (S, 0, 6), (L, 0, 7), (L, 1, 5), (S, 1, 5),
-        (S, 0, 7), (O, 6), (O, 7), (L, 3, 0), (re, 5), (db, 6), (da, 7), (pn, 4), (L, 2, 1), (S, 2, 1), (L, 2, 2),
-        (S, 2, 2), (fa, 4), (L, 2, 3), (S, 2, 3), (L, 2, 4), (S, 2, 4), (ne, 5), (L, 1, 6), (pf, 4), (L, 0, 8),
-        (S, 0, 8), (L, 0, 9), (S, 1, 6), (L, 1, 7), (S, 0, 9), (O, 8), (O, 9), (re, 6), (db, 7), (da, 8), (L, 2, 5),
-        (S, 2, 5), (pn, 5), (L, 3, 1), (L, 3, 2), (S, 1, 7), (fa, 5), (F, 0), (L, 3, 3), (L, 3, 4), (ne, 6),
-        (L, 2, 6), (pf, 5), (S, 1, 8), (L, 0, 10), (S, 0, 10), (L, 0, 11), (S, 0, 11), (O, 10), (L, 1, 8), (O, 11),
-        (S, 2, 6), (re, 7), (db, 8), (L, 1, 9), (S, 1, 9), (pn, 6), (L, 2, 7), (fa, 6), (L, 3, 5), (S, 2, 7),
-        (ne, 7), (F, 1), (S, 2, 8), (pf, 6), (F, 2), (F, 3), (L, 3, 6), (S, 1, 10), (L, 0, 12), (S, 0, 12),
-        (L, 0, 13), (S, 0, 13), (F, 4), (O, 12), (O, 13), (re, 8), (S, 1, 11), (L, 1, 10), (pn, 7), (L, 1, 11),
-        (fa, 7), (L, 2, 8), (S, 2, 9), (L, 2, 9), (ne, 8), (L, 3, 7), (pf, 7), (L, 0, 14), (S, 0, 14), (L, 0, 15),
-        (S, 0, 15), (S, 2, 10), (O, 14), (O, 15), (S, 1, 12), (fa, 8), (F, 5), (pn, 8), (F, 6), (S, 2, 11),
-        (L, 1, 12), (L, 1, 13), (S, 1, 13), (pf, 8), (L, 0, 16), (S, 0, 16), (L, 2, 10), (L, 0, 17), (S, 0, 17),
-        (pb,), (L, 3, 8), (L, 2, 11), (S, 1, 14), (S, 1, 15), (L, 3, 9), (L, 0, 18), (S, 0, 18), (L, 0, 19),
-        (S, 0, 19), (L, 0, 20), (S, 0, 20), (O, 16), (O, 17), (O, 18), (O, 19), (O, 20), (S, 2, 12), (L, 1, 14),
-        (F, 7), (L, 0, 21), (S, 0, 21), (O, 21), (S, 2, 13), (L, 1, 15), (L, 2, 12), (S, 1, 16), (L, 2, 13),
-        (S, 1, 17), (S, 2, 14), (L, 1, 16), (L, 3, 10), (S, 2, 15), (L, 1, 17), (S, 1, 18), (S, 1, 19), (L, 3, 11),
-        (S, 1, 20), (F, 8), (L, 1, 18), (S, 1, 21), (F, 9), (L, 1, 19), (S, 2, 16), (L, 1, 20), (L, 2, 14),
-        (S, 2, 17), (L, 1, 21), (L, 2, 15), (L, 3, 12), (S, 2, 18), (L, 3, 13), (S, 2, 19), (L, 2, 16), (S, 2, 20),
-        (S, 2, 21), (L, 2, 17), (F, 10), (L, 2, 18), (F, 11), (L, 2, 19), (L, 2, 20), (L, 3, 14), (L, 2, 21),
-        (L, 3, 15), (L, 3, 16), (F, 12), (L, 3, 17), (F, 13), (L, 3, 18), (L, 3, 19), (L, 3, 20), (L, 3, 21),
-        (F, 14), (F, 15), (F, 16), (F, 17), (F, 18), (F, 19), (F, 20), (F, 21),
+        (sx, 0), (sx, 1), (st, 0), (sx, 2), (sx, 3), (sx, 4), (sx, 5), (ax, 0), (da, 0), (db, 0), (st, 1), (sx, 6),
+        (sx, 7), (ax, 1), (da, 1), (ax, 2), (ow, 0), (ax, 3), (re, 0), (db, 1), (da, 2), (ax, 4), (ow, 1), (ne, 0),
+        (ax, 5), (re, 1), (db, 2), (da, 3), (ow, 2), (ax, 6), (fa, 0), (st, 2), (pn, 0, 0), (ax, 7), (pv,), (ne, 1),
+        (pf, 0, 0), (L, 0, 0), (S, 0, 0), (O, 0), (re, 2), (db, 3), (da, 4), (ow, 3), (pa, 0, 1), (L, 0, 1),
+        (S, 0, 1), (pn, 1, 0), (fa, 1), (O, 1), (ne, 2), (L, 1, 0), (S, 1, 0), (pf, 1, 0), (L, 0, 2), (S, 0, 2),
+        (pa, 1, 1), (re, 3), (db, 4), (da, 5), (L, 1, 1), (S, 1, 1), (L, 0, 3), (S, 0, 3), (O, 2), (O, 3), (pn, 2),
+        (fa, 2), (L, 2, 0), (S, 2, 0), (ne, 3), (L, 1, 2), (S, 1, 2), (pf, 2), (L, 0, 4), (S, 0, 4), (L, 0, 5),
+        (L, 2, 1), (S, 2, 1), (S, 0, 5), (O, 4), (O, 5), (re, 4), (db, 5), (da, 6), (L, 1, 3), (S, 1, 3), (pn, 3),
+        (fa, 3), (L, 3, 0), (L, 2, 2), (S, 2, 2), (ne, 4), (L, 1, 4), (S, 1, 4), (pf, 3), (L, 1, 5), (L, 0, 6),
+        (S, 0, 6), (L, 0, 7), (S, 0, 7), (O, 6), (O, 7), (re, 5), (db, 6), (da, 7), (L, 3, 1), (S, 1, 5), (pn, 4),
+        (fa, 4), (L, 2, 3), (S, 2, 3), (L, 3, 2), (S, 2, 4), (ne, 5), (F, 0), (L, 2, 4), (S, 1, 6), (pf, 4),
+        (L, 0, 8), (S, 0, 8), (L, 0, 9), (L, 2, 5), (S, 1, 7), (S, 0, 9), (O, 8), (O, 9), (re, 6), (db, 7),
+        (L, 1, 6), (S, 2, 5), (pn, 5), (fa, 5), (L, 1, 7), (L, 3, 3), (S, 2, 6), (ne, 6), (F, 1), (pf, 5), (S, 1, 8),
+        (L, 0, 10), (S, 0, 10), (L, 0, 11), (S, 0, 11), (L, 3, 4), (O, 10), (S, 2, 7), (re, 7), (O, 11), (F, 2),
+        (L, 1, 8), (S, 1, 9), (pn, 6), (fa, 6), (L, 1, 9), (L, 3, 5), (L, 2, 6), (ne, 7), (S, 2, 8), (L, 2, 7),
+        (pf, 6), (S, 1, 10), (L, 0, 12), (S, 0, 12), (L, 0, 13), (S, 0, 13), (O, 12), (O, 13), (S, 1, 11),
+        (L, 1, 10), (fa, 7), (pn, 7), (F, 3), (L, 1, 11), (S, 2, 9), (pf, 7), (L, 2, 8), (L, 0, 14), (S, 0, 14),
+        (L, 0, 15), (F, 4), (S, 2, 10), (S, 0, 15), (pb,), (L, 3, 6), (L, 2, 9), (S, 1, 12), (S, 1, 13), (L, 0, 16),
+        (S, 0, 16), (F, 5), (S, 2, 11), (L, 3, 7), (L, 0, 17), (S, 0, 17), (L, 0, 18), (S, 0, 18), (L, 0, 19),
+        (S, 0, 19), (O, 14), (O, 15), (O, 16), (O, 17), (O, 18), (O, 19), (L, 1, 12), (S, 1, 14), (L, 1, 13),
+        (L, 2, 10), (S, 1, 15), (L, 2, 11), (S, 2, 12), (L, 3, 8), (S, 2, 13), (L, 1, 14), (S, 1, 16), (L, 1, 15),
+        (S, 1, 17), (L, 3, 9), (F, 6), (S, 1, 18), (L, 1, 16), (S, 1, 19), (S, 2, 14), (L, 1, 17), (F, 7),
+        (S, 2, 15), (L, 1, 18), (L, 1, 19), (L, 2, 12), (S, 2, 16), (L, 2, 13), (S, 2, 17), (L, 3, 10), (S, 2, 18),
+        (L, 3, 11), (S, 2, 19), (L, 2, 14), (F, 8), (L, 2, 15), (L, 2, 16), (F, 9), (L, 2, 17), (L, 2, 18),
+        (L, 2, 19), (L, 3, 12), (L, 3, 13), (L, 3, 14), (L, 3, 15), (F, 10), (F, 11), (L, 3, 16), (L, 3, 17),
+        (L, 3, 18), (L, 3, 19), (F, 12), (F, 13), (F, 14), (F, 15), (F, 16), (F, 17), (F, 18), (F, 19),
     ]
     for step, *at in plan:
         with jax.named_scope("_".join((step.__name__, *map(str, at)))):
@@ -521,9 +510,9 @@
             dma((4,)),
             dma, dma((n,)), dma((2,)), dma,
             dma, dma, dma, dma, dma((2,)), dma((2,)),
-            dma, dma((n, 2)), dma, dma((n,)), dma, dma((n, 3)),
+            dma, dma((1 + max(map(max, SIDE_AT)),)), dma, dma, dma((1 + max(map(max, CORE_AT)),)),
             dma, dma((1 + max(map(max, LONG_AT)),)), dma, dma((1 + max(map(max, SHORT_AT)),)),
-            dma, dma((2,)), dma((len(PARTS), 2)),
+            dma, dma((2,)), dma((ENDS, 2)),
         ],
         compiler_params=pltpu.CompilerParams(has_side_effects=True, collective_id=0, vmem_limit_bytes=44 * 2**20),
     )(pltpu.with_memory_space_constraint(dosages, pltpu.HBM))

time: 86.6 us -> 84.3 us (0.973)
  Pallas kernels: 84.2 us -> 81.8 us
    pallas_call x1, Pallas kernels: 84.2 us -> 81.8 us  [shards(): pl.pallas_call(kernel, name='ld', out_shape=(jax.ShapeDtypeStruct((1, 256...]
where the time goes in v2:
time: 84.3 us; the launch traced here: 84.1 us
  Pallas kernels  81.8 us (97%)
  local copies, waits for them, and re-layouts  1.67 us (2%)
    pallas_call x1, Pallas kernels, shards(): pl.pallas_call(kernel, name='ld', out_shape=(jax.ShapeDtypeStruct((1, 256...  81.8 us

profile of v2, /device:TPU:1, one launch (start us, length us, event | category | flops | bytes accessed | tf_op | source)
XLA Modules:
  0.0 84.1 jit_solution(3973215171661555213)
XLA Ops:
  0.6 81.8 %ld.1 = (f32[1,256,1024]{2,1,0:T(8,128)S(1)}, f32[1,64,1024]{2,1,0:T(8,128)S(1)}) custom-call(bf16[512,1024]{1,0:T(8,128)(2,1)} %x_hbm.1), custom_call_target="tpu_custom_call" | custom-call | tf_op jit(solution)/shard_map/ld/pallas_call | solution.py:482
  82.4 1.0 %copy.5 = f32[1,256,1024]{2,1,0:T(8,128)} copy(f32[1,256,1024]{2,1,0:T(8,128)S(1)} %get-tuple-element.4) | data formatting | bytes 2097152
  83.4 0.7 copy.6

commit v3 on v2

--- a/solution.py
+++ b/solution.py
@@ -15,34 +15,35 @@
 FLOOR = 0.05
 POWER = 15
 SCALE = 2.0 ** (126.5 / POWER)
-FIRST = (0, 64, 128, 192, 256, 320, 384, 448)
-ROWS = (64, 64, 64, 64, 64, 64, 64, 64)
+FIRST = (0, 32, 64, 128, 192, 256, 320, 384, 448)
+ROWS = (32, 32, 64, 64, 64, 64, 64, 64, 64)
 PARTS = (
-    (0, 64, 0, 256), (0, 64, 256, 256), (64, 64, 0, 256), (64, 64, 256, 256), (128, 32, 0, 512), (160, 32, 0, 512),
-    (192, 32, 0, 512), (224, 32, 0, 512), (256, 32, 0, 512), (288, 32, 0, 512), (320, 32, 0, 512),
-    (352, 32, 0, 512), (384, 32, 0, 512), (416, 32, 0, 512), (448, 32, 0, 512), (480, 32, 0, 512),
-    (576, 32, 0, 512), (608, 32, 0, 512), (512, 32, 0, 512), (544, 32, 0, 512),
+    (0, 32, 0, 256), (0, 32, 256, 256), (32, 32, 0, 256), (32, 32, 256, 256), (64, 64, 0, 256), (64, 64, 256, 256),
+    (128, 32, 0, 512), (160, 32, 0, 512), (192, 32, 0, 512), (224, 32, 0, 512), (256, 32, 0, 512),
+    (288, 32, 0, 512), (320, 32, 0, 512), (352, 32, 0, 512), (384, 32, 0, 512), (416, 32, 0, 512),
+    (448, 32, 0, 512), (480, 32, 0, 512), (576, 32, 0, 512), (608, 32, 0, 512), (512, 32, 0, 512),
+    (544, 32, 0, 512),
 )
 ENDS = max(sum((r // 256 if r < 512 else (r - 512) // 64) == h for r, _, _, _ in PARTS) for h in range(2))
 TURN = sum(row < 128 for row in FIRST)
 LONG_AT = (
-    (0, 1, 3, 5, 7, 8, 11, 12, 8, 6, 1, 2, 11, 12, 8, 16, 6, 7, 9, 17),
-    (2, 4, 0, 1, 2, 3, 5, 9, 3, 10, 14, 15, 18, 1, 10, 13, 4, 11, 12, 14),
-    (6, 9, 10, 4, 0, 7, 13, 4, 0, 5, 2, 3, 19, 0, 6, 5, 16, 8, 15, 20),
+    (0, 2, 3, 4, 5, 6, 12, 13, 2, 15, 8, 9, 1, 3, 15, 16, 7, 17, 8, 9, 10, 1),
+    (1, 0, 8, 9, 10, 11, 6, 16, 10, 11, 4, 5, 14, 0, 11, 13, 5, 2, 6, 4, 15, 0),
+    (7, 14, 1, 3, 4, 5, 0, 13, 6, 2, 12, 18, 19, 3, 14, 16, 18, 8, 9, 7, 12, 17),
 )
 SHORT_AT = (
-    (0, 1, 3, 5, 6, 7, 2, 8, 5, 4, 10, 11, 8, 1, 6, 0, 12, 7, 13, 14),
-    (2, 4, 0, 1, 3, 9, 0, 6, 7, 2, 9, 3, 4, 5, 10, 11, 2, 15, 9, 1),
+    (0, 2, 3, 4, 5, 6, 11, 12, 5, 4, 10, 9, 0, 2, 5, 12, 9, 8, 10, 1, 13, 0),
+    (1, 0, 7, 8, 9, 10, 6, 3, 8, 11, 7, 6, 3, 4, 11, 14, 7, 2, 6, 15, 16, 3),
 )
 SIDE_AT = (
-    (0, 2, 5, 8, 10, 11, 4, 7),
-    (1, 4, 7, 9, 1, 3, 6, 0),
-    (3, 6, 0, 2, 5, 8, 10, 11),
+    (0, 2, 4, 8, 11, 1, 12, 6, 10),
+    (1, 3, 7, 10, 0, 3, 5, 9, 0),
+    (5, 6, 9, 2, 4, 8, 11, 1, 12),
 )
 CORE_AT = (
-    (0, 1, 2, 3, 4, 1, 2, 5),
-    (0, 6, 1, 3, 1, 3, 1, 3),
-    (3, 0, 2, 0, 2, 0, 2, 0),
+    (0, 1, 2, 3, 4, 0, 2, 8, 6),
+    (5, 6, 5, 0, 6, 7, 6, 7, 6),
+    (1, 7, 7, 5, 0, 5, 0, 5, 0),
 )
 
 bf16, f32 = jnp.bfloat16, jnp.float32
@@ -420,32 +421,35 @@
                     band_ref[0, pl.ds((row - 512) % 64, tall), there] = value
 
     plan = [
-        (sx, 0), (sx, 1), (st, 0), (sx, 2), (sx, 3), (sx, 4), (sx, 5), (ax, 0), (da, 0), (db, 0), (st, 1), (sx, 6),
-        (sx, 7), (ax, 1), (da, 1), (ax, 2), (ow, 0), (ax, 3), (re, 0), (db, 1), (da, 2), (ax, 4), (ow, 1), (ne, 0),
-        (ax, 5), (re, 1), (db, 2), (da, 3), (ow, 2), (ax, 6), (fa, 0), (st, 2), (pn, 0, 0), (ax, 7), (pv,), (ne, 1),
-        (pf, 0, 0), (L, 0, 0), (S, 0, 0), (O, 0), (re, 2), (db, 3), (da, 4), (ow, 3), (pa, 0, 1), (L, 0, 1),
-        (S, 0, 1), (pn, 1, 0), (fa, 1), (O, 1), (ne, 2), (L, 1, 0), (S, 1, 0), (pf, 1, 0), (L, 0, 2), (S, 0, 2),
-        (pa, 1, 1), (re, 3), (db, 4), (da, 5), (L, 1, 1), (S, 1, 1), (L, 0, 3), (S, 0, 3), (O, 2), (O, 3), (pn, 2),
-        (fa, 2), (L, 2, 0), (S, 2, 0), (ne, 3), (L, 1, 2), (S, 1, 2), (pf, 2), (L, 0, 4), (S, 0, 4), (L, 0, 5),
-        (L, 2, 1), (S, 2, 1), (S, 0, 5), (O, 4), (O, 5), (re, 4), (db, 5), (da, 6), (L, 1, 3), (S, 1, 3), (pn, 3),
-        (fa, 3), (L, 3, 0), (L, 2, 2), (S, 2, 2), (ne, 4), (L, 1, 4), (S, 1, 4), (pf, 3), (L, 1, 5), (L, 0, 6),
-        (S, 0, 6), (L, 0, 7), (S, 0, 7), (O, 6), (O, 7), (re, 5), (db, 6), (da, 7), (L, 3, 1), (S, 1, 5), (pn, 4),
-        (fa, 4), (L, 2, 3), (S, 2, 3), (L, 3, 2), (S, 2, 4), (ne, 5), (F, 0), (L, 2, 4), (S, 1, 6), (pf, 4),
-        (L, 0, 8), (S, 0, 8), (L, 0, 9), (L, 2, 5), (S, 1, 7), (S, 0, 9), (O, 8), (O, 9), (re, 6), (db, 7),
-        (L, 1, 6), (S, 2, 5), (pn, 5), (fa, 5), (L, 1, 7), (L, 3, 3), (S, 2, 6), (ne, 6), (F, 1), (pf, 5), (S, 1, 8),
-        (L, 0, 10), (S, 0, 10), (L, 0, 11), (S, 0, 11), (L, 3, 4), (O, 10), (S, 2, 7), (re, 7), (O, 11), (F, 2),
-        (L, 1, 8), (S, 1, 9), (pn, 6), (fa, 6), (L, 1, 9), (L, 3, 5), (L, 2, 6), (ne, 7), (S, 2, 8), (L, 2, 7),
-        (pf, 6), (S, 1, 10), (L, 0, 12), (S, 0, 12), (L, 0, 13), (S, 0, 13), (O, 12), (O, 13), (S, 1, 11),
-        (L, 1, 10), (fa, 7), (pn, 7), (F, 3), (L, 1, 11), (S, 2, 9), (pf, 7), (L, 2, 8), (L, 0, 14), (S, 0, 14),
-        (L, 0, 15), (F, 4), (S, 2, 10), (S, 0, 15), (pb,), (L, 3, 6), (L, 2, 9), (S, 1, 12), (S, 1, 13), (L, 0, 16),
-        (S, 0, 16), (F, 5), (S, 2, 11), (L, 3, 7), (L, 0, 17), (S, 0, 17), (L, 0, 18), (S, 0, 18), (L, 0, 19),
-        (S, 0, 19), (O, 14), (O, 15), (O, 16), (O, 17), (O, 18), (O, 19), (L, 1, 12), (S, 1, 14), (L, 1, 13),
-        (L, 2, 10), (S, 1, 15), (L, 2, 11), (S, 2, 12), (L, 3, 8), (S, 2, 13), (L, 1, 14), (S, 1, 16), (L, 1, 15),
-        (S, 1, 17), (L, 3, 9), (F, 6), (S, 1, 18), (L, 1, 16), (S, 1, 19), (S, 2, 14), (L, 1, 17), (F, 7),
-        (S, 2, 15), (L, 1, 18), (L, 1, 19), (L, 2, 12), (S, 2, 16), (L, 2, 13), (S, 2, 17), (L, 3, 10), (S, 2, 18),
-        (L, 3, 11), (S, 2, 19), (L, 2, 14), (F, 8), (L, 2, 15), (L, 2, 16), (F, 9), (L, 2, 17), (L, 2, 18),
-        (L, 2, 19), (L, 3, 12), (L, 3, 13), (L, 3, 14), (L, 3, 15), (F, 10), (F, 11), (L, 3, 16), (L, 3, 17),
-        (L, 3, 18), (L, 3, 19), (F, 12), (F, 13), (F, 14), (F, 15), (F, 16), (F, 17), (F, 18), (F, 19),
+        (sx, 0), (sx, 1), (sx, 2), (st, 0), (sx, 3), (sx, 4), (ax, 0), (da, 0), (db, 0), (ax, 1), (da, 1), (db, 1),
+        (st, 1), (sx, 5), (sx, 6), (sx, 7), (sx, 8), (ax, 2), (da, 2), (ax, 3), (ow, 0), (re, 0), (ax, 4), (ne, 0),
+        (re, 1), (db, 2), (da, 3), (ne, 1), (ow, 1), (ax, 5), (st, 2), (re, 2), (db, 3), (da, 4), (fa, 0),
+        (pn, 0, 0), (ax, 6), (pn, 1, 0), (fa, 1), (ax, 7), (pf, 0, 0), (L, 0, 0), (S, 0, 0), (O, 0), (ow, 2),
+        (ne, 2), (pf, 1, 0), (ax, 8), (pv,), (re, 3), (db, 4), (da, 5), (pn, 2, 0), (ow, 3), (L, 1, 0), (fa, 2),
+        (S, 1, 0), (pa, 0, 1), (L, 0, 1), (S, 0, 1), (L, 0, 2), (S, 0, 2), (pa, 1, 1), (L, 0, 3), (ne, 3), (S, 0, 3),
+        (O, 1), (O, 2), (O, 3), (pf, 2, 0), (L, 0, 4), (S, 0, 4), (pa, 2, 1), (re, 4), (db, 5), (da, 6), (L, 0, 5),
+        (S, 0, 5), (L, 2, 0), (S, 2, 0), (O, 4), (O, 5), (pn, 3), (fa, 3), (L, 1, 1), (S, 1, 1), (L, 1, 2),
+        (S, 1, 2), (L, 1, 3), (S, 1, 3), (ne, 4), (L, 1, 4), (S, 1, 4), (pf, 3), (L, 1, 5), (S, 1, 5), (L, 0, 6),
+        (S, 0, 6), (L, 0, 7), (L, 3, 0), (S, 0, 7), (O, 6), (O, 7), (re, 5), (db, 6), (da, 7), (L, 2, 1), (S, 2, 1),
+        (L, 2, 2), (pn, 4), (fa, 4), (S, 2, 2), (L, 2, 3), (S, 2, 3), (L, 2, 4), (S, 2, 4), (ne, 5), (L, 2, 5),
+        (S, 2, 5), (pf, 4), (L, 1, 6), (S, 1, 6), (L, 0, 8), (S, 0, 8), (L, 0, 9), (S, 0, 9), (O, 8), (O, 9),
+        (re, 6), (db, 7), (da, 8), (L, 1, 7), (S, 1, 7), (pn, 5), (fa, 5), (L, 3, 1), (L, 3, 2), (L, 3, 3), (F, 0),
+        (L, 3, 4), (ne, 6), (L, 3, 5), (pf, 5), (S, 2, 6), (L, 2, 6), (L, 0, 10), (S, 0, 10), (L, 0, 11), (S, 0, 11),
+        (O, 10), (O, 11), (re, 7), (db, 8), (S, 1, 8), (L, 1, 8), (pn, 6), (fa, 6), (L, 1, 9), (S, 2, 7), (L, 2, 7),
+        (S, 1, 9), (ne, 7), (F, 1), (F, 2), (F, 3), (pf, 6), (S, 1, 10), (L, 0, 12), (S, 0, 12), (L, 0, 13), (F, 4),
+        (S, 0, 13), (re, 8), (L, 3, 6), (O, 12), (S, 1, 11), (O, 13), (F, 5), (L, 1, 10), (pn, 7), (fa, 7),
+        (S, 2, 8), (L, 1, 11), (L, 2, 8), (S, 2, 9), (ne, 8), (L, 2, 9), (S, 2, 10), (pf, 7), (L, 3, 7), (S, 1, 12),
+        (L, 0, 14), (S, 0, 14), (L, 0, 15), (S, 0, 15), (O, 14), (O, 15), (L, 1, 12), (S, 1, 13), (fa, 8), (pn, 8),
+        (S, 2, 11), (L, 1, 13), (L, 2, 10), (pf, 8), (F, 6), (L, 0, 16), (S, 0, 16), (L, 0, 17), (L, 2, 11),
+        (S, 0, 17), (pb,), (L, 3, 8), (L, 3, 9), (S, 2, 12), (S, 1, 14), (L, 0, 18), (S, 0, 18), (L, 0, 19),
+        (S, 0, 19), (L, 0, 20), (S, 0, 20), (S, 1, 15), (O, 16), (O, 17), (O, 18), (O, 19), (O, 20), (L, 1, 14),
+        (S, 2, 13), (F, 7), (L, 0, 21), (S, 0, 21), (O, 21), (L, 1, 15), (L, 2, 12), (S, 1, 16), (L, 2, 13),
+        (S, 1, 17), (L, 3, 10), (L, 1, 16), (S, 2, 14), (L, 1, 17), (S, 1, 18), (L, 3, 11), (S, 1, 19), (S, 1, 20),
+        (S, 2, 15), (F, 8), (L, 1, 18), (F, 9), (L, 1, 19), (S, 1, 21), (L, 1, 20), (S, 2, 16), (L, 2, 14),
+        (S, 2, 17), (L, 1, 21), (L, 2, 15), (S, 2, 18), (L, 3, 12), (S, 2, 19), (L, 3, 13), (S, 2, 20), (L, 2, 16),
+        (S, 2, 21), (F, 10), (L, 2, 17), (L, 2, 18), (F, 11), (L, 2, 19), (L, 2, 20), (L, 3, 14), (L, 2, 21),
+        (L, 3, 15), (L, 3, 16), (L, 3, 17), (F, 12), (L, 3, 18), (F, 13), (L, 3, 19), (L, 3, 20), (L, 3, 21),
+        (F, 14), (F, 15), (F, 16), (F, 17), (F, 18), (F, 19), (F, 20), (F, 21),
     ]
     for step, *at in plan:
         with jax.named_scope("_".join((step.__name__, *map(str, at)))):

time: 84.3 us -> 84 us (level)
  no operation moved by 1% of the time
where the time goes in v3:
time: 84 us; the launch traced here: 83.9 us
  Pallas kernels  81.6 us (97%)
  local copies, waits for them, and re-layouts  1.67 us (2%)
    pallas_call x1, Pallas kernels, shards(): pl.pallas_call(kernel, name='ld', out_shape=(jax.ShapeDtypeStruct((1, 256...  81.6 us

profile of v3, /device:TPU:1, one launch (start us, length us, event | category | flops | bytes accessed | tf_op | source)
XLA Modules:
  0.0 83.9 jit_solution(4376908313674550853)
XLA Ops:
  0.6 81.6 %ld.1 = (f32[1,256,1024]{2,1,0:T(8,128)S(1)}, f32[1,64,1024]{2,1,0:T(8,128)S(1)}) custom-call(bf16[512,1024]{1,0:T(8,128)(2,1)} %x_hbm.1), custom_call_target="tpu_custom_call" | custom-call | tf_op jit(solution)/shard_map/ld/pallas_call | solution.py:486
  82.2 1.0 %copy.5 = f32[1,256,1024]{2,1,0:T(8,128)} copy(f32[1,256,1024]{2,1,0:T(8,128)S(1)} %get-tuple-element.4) | data formatting | bytes 2097152
  83.2 0.7 copy.6

commit v4 on v3

--- a/solution.py
+++ b/solution.py
@@ -343,7 +343,7 @@
             return remote(long_out.at[t, r, c], long_in.at[t, r, c], l_send, l_recv.at[LONG_AT[t][u]], fwd)
         hr, hc = at_home(u)
         return remote(
-            long_out.at[t, r, c], ends.at[0, core, hr, hc], l_send, e_recv.at[slot(u), core],
+            long_out.at[t, r, c], ends.at[0, core, hr, hc], l_send, e_recv.at[slot(u)],
             home(u, (z + 8 + sign) % Z),
         )
 
@@ -353,7 +353,7 @@
             return remote(short_out.at[t, r, c], short_in.at[t, r, c], t_send, t_recv.at[SHORT_AT[t][u]], bwd)
         hr, hc = at_home(u)
         return remote(
-            short_out.at[t, r, c], ends.at[1, core, hr, hc], t_send, e_recv.at[slot(u), core],
+            short_out.at[t, r, c], ends.at[1, core, hr, hc], t_send, e_recv.at[slot(u)],
             home(u, (z + 8 - sign) % Z),
         )
 
@@ -387,7 +387,7 @@
         main_part = PARTS[u][0] < 512
         copy = remote(
             own_out.at[r, c], ends.at[2, core, hr, hc], o_send if main_part else b_send.at[half_of(u)],
-            e_recv.at[slot(u), core], home(u, z),
+            e_recv.at[slot(u)], home(u, z),
         )
         if local_end(u):
             pl.when(jnp.logical_not(to_self))(copy.start)
@@ -403,15 +403,15 @@
         def _():
             row, tall, col, wide = PARTS[u]
             hr, hc = at_home(u)
+            if local_end(u):
+                pl.when(to_self)(lambda: bytes_of(ends.at[0, 0, pl.ds(0, 5 * tall), pl.ds(0, wide)], e_recv.at[slot(u)]))
+
+                @pl.when(jnp.logical_not(to_self))
+                def _():
+                    bytes_of(ends.at[:, :, pl.ds(0, tall), pl.ds(0, wide)], e_recv.at[slot(u)])
+            else:
+                bytes_of(ends.at[:, :, pl.ds(0, tall), pl.ds(0, wide)], e_recv.at[slot(u)])
             for c in range(2):
-                def arrived(n):
-                    bytes_of(ends.at[0, 0, pl.ds(0, n * tall), pl.ds(0, wide)], e_recv.at[slot(u), c])
-
-                if local_end(u) and c == 1:
-                    pl.when(to_self)(lambda: arrived(2))
-                    pl.when(jnp.logical_not(to_self))(lambda: arrived(3))
-                else:
-                    arrived(3)
                 w = sum(decoded(ends[n, c, hr, hc]) for n in range(3))
                 value = w * w * (1.0 / (SCALE * SCALE))
                 there = pl.ds(HALF * c + col, wide)
@@ -516,7 +516,7 @@
             dma, dma, dma, dma, dma((2,)), dma((2,)),
             dma, dma((1 + max(map(max, SIDE_AT)),)), dma, dma, dma((1 + max(map(max, CORE_AT)),)),
             dma, dma((1 + max(map(max, LONG_AT)),)), dma, dma((1 + max(map(max, SHORT_AT)),)),
-            dma, dma((2,)), dma((ENDS, 2)),
+            dma, dma((2,)), dma((ENDS,)),
         ],
         compiler_params=pltpu.CompilerParams(has_side_effects=True, collective_id=0, vmem_limit_bytes=44 * 2**20),
     )(pltpu.with_memory_space_constraint(dosages, pltpu.HBM))

time: 84 us -> 83.9 us (level)
  no operation moved by 1% of the time
where the time goes in v4:
time: 83.9 us; the launch traced here: 83.8 us
  Pallas kernels  81.5 us (97%)
  local copies, waits for them, and re-layouts  1.67 us (2%)
    pallas_call x1, Pallas kernels, shards(): pl.pallas_call(kernel, name='ld', out_shape=(jax.ShapeDtypeStruct((1, 256...  81.5 us

profile of v4, /device:TPU:1, one launch (start us, length us, event | category | flops | bytes accessed | tf_op | source)
XLA Modules:
  0.0 83.8 jit_solution(5126506294136209492)
XLA Ops:
  0.6 81.5 %ld.1 = (f32[1,256,1024]{2,1,0:T(8,128)S(1)}, f32[1,64,1024]{2,1,0:T(8,128)S(1)}) custom-call(bf16[512,1024]{1,0:T(8,128)(2,1)} %x_hbm.1), custom_call_target="tpu_custom_call" | custom-call | tf_op jit(solution)/shard_map/ld/pallas_call | solution.py:486
  82.2 1.0 %copy.5 = f32[1,256,1024]{2,1,0:T(8,128)} copy(f32[1,256,1024]{2,1,0:T(8,128)S(1)} %get-tuple-element.4) | data formatting | bytes 2097152
  83.1 0.7 copy.6
